TPU v7x, 32 devices: a whole 2x2x4 slice. The times are simulated.
32 devices in a mesh: gx: 2 (over x), gy: 4 (over z), gz: 4 (over y, core).
Axes of the slice: x: 2, y: 2, z: 4, core: 2. Of those that a mesh axis runs over, the one named last changes fastest.
Arguments:
- calcium: float32 [8, 64, 128, 512], P(None, 'gx', 'gz', 'gy'), may hold values from 0.1 to 3
- activation: float32 [8, 64, 128, 512], P(None, 'gx', 'gz', 'gy'), may hold values from 0 to 1
- element_first: int32 [64], replicated, may hold values from 0 to 15, as said below
- offset_first: float32 [64], replicated, may hold values from 0.1 to 0.9
- element_second: int32 [512], replicated, may hold values from 0 to 127, as said below
- offset_second: float32 [512], replicated, may hold values from 0.1 to 0.9
- element_third: int32 [128], replicated, may hold values from 0 to 31, as said below
- offset_third: float32 [128], replicated, may hold values from 0.1 to 0.9
- troponin: float32 [16, 32, 128], P('gx', ('gy', 'gz')), may hold values from 0 to 1
- tension: float32 [16, 32, 128], P('gx', ('gy', 'gz')), may hold values from 0 to 2
- unbind_rate: float32 [16, 32, 128], P('gx', ('gy', 'gz')), may hold values from 0.2 to 2
- relax_rate: float32 [16, 32, 128], P('gx', ('gy', 'gz')), may hold values from 0.5 to 4
Outputs:
- bound_fraction: float32 [16, 32, 128], P('gx', ('gy', 'gz'))
- active_tension: float32 [16, 32, 128], P('gx', ('gy', 'gz'))
Inputs may be any that keep to these rules, and one draw needn't show every extreme that they name: `element_first`: never falling; the cells of each aligned block of 32 cells belong to that block's own 8 elements, each element holding at least one cell. `element_second`: never falling; the cells of each aligned block of 128 cells belong to that block's own 32 elements, each element holding at least one cell. `element_third`: never falling; the cells of each aligned block of 8 cells belong to that block's own 2 elements, each element holding at least one cell.
All inputs are finite; a program needn't handle non-finite values.
Results may differ from a plain program's by a relative error of at most 0.00005.
Values sent between devices are 32-bit elements.
A program may use at most 64 MiB of HBM per device.

v0:
```python
import functools

import jax
import jax.numpy as jnp
from jax import lax
from jax.experimental import pallas as pl
from jax.experimental.pallas import tpu as pltpu
from jax.sharding import PartitionSpec as P

step_size = 0.2
bind_rate = 2.0
peak_tension = 2.0
half_square = 0.25
f32 = jnp.float32
bf16 = jnp.bfloat16
MESH = pl.DeviceIdType.MESH
CHUNKS = 2


def split(x):
    high = x.astype(bf16)
    return high, (x - high.astype(f32)).astype(bf16)


def node_weights(element, offset, node):
    raw = jnp.where(element == node, 1.0 - offset, 0.0) + jnp.where(
        element + 1 == node, offset, 0.0
    )
    total = jnp.sum(raw, axis=1, keepdims=True)
    return raw, jnp.where(total > 0.0, total, 1.0)


def expand(weight, pick):
    high, low = split(weight)
    return jnp.dot(high, pick, preferred_element_type=f32) + jnp.dot(
        low, pick, preferred_element_type=f32
    )


def iota(shape, dim):
    return lax.broadcasted_iota(jnp.int32, shape, dim)


def kernel(
    calcium,
    activation,
    *refs,
    sizes,
):
    small = refs[:10]
    out_bound, out_active, xc, xa = refs[10:14]
    local = refs[14:24]
    (
        main,
        third,
        edge,
        got_main,
        got_third,
        got_first,
        got_corner,
        load_sem,
        small_sem,
        send_main,
        send_edge,
        recv_main,
        recv_third,
        recv_first,
        recv_corner,
    ) = refs[24:]
    e1, o1, e2, o2, e3, o3, troponin, tension, unbind, relax = local
    nx, ny, nz = sizes
    subs, rows, depth, cols = xc.shape
    nodes_x, per_block, all_y = troponin.shape
    nodes_y = all_y // ny
    blocks = nz
    slab = per_block * blocks
    gx, gy, gz = lax.axis_index("gx"), lax.axis_index("gy"), lax.axis_index("gz")
    chunk = subs // CHUNKS

    def load(t):
        return (
            pltpu.make_async_copy(calcium.at[t], xc.at[t], load_sem.at[0, t]),
            pltpu.make_async_copy(activation.at[t], xa.at[t], load_sem.at[1, t]),
        )

    fetches = [
        pltpu.make_async_copy(source, target, small_sem.at[i])
        for i, (source, target) in enumerate(zip(small, local))
    ]
    for copy in fetches:
        copy.start()
    for t in range(subs):
        for copy in load(t):
            copy.start()

    barrier = pltpu.get_barrier_semaphore()
    has_next_x = gx + 1 < nx
    has_next_z = gz + 1 < nz
    own = gy == gz
    from_third = jnp.logical_and(gz == 0, gy > 0)
    from_first = gx > 0
    from_corner = jnp.logical_and(from_third, from_first)
    for s in range(ny):

        def greet(dx, dz, s=s):
            pl.semaphore_signal(
                barrier, inc=1, device_id=(gx - dx, s, gy - dz), device_id_type=MESH
            )

        @pl.when(jnp.logical_not(jnp.logical_and(s == gy, own)))
        def _():
            greet(0, 0)

        @pl.when(jnp.logical_and(from_third, jnp.logical_not(jnp.logical_and(s == gy, gy - 1 == gz))))
        def _():
            greet(0, 1)

        @pl.when(from_first)
        def _():
            greet(1, 0)

        @pl.when(from_corner)
        def _():
            greet(1, 1)

    for copy in fetches[:6]:
        copy.wait()
    row_count = (slab + 1) * nodes_x + 16
    r = iota((row_count, 1), 0)
    inner = r < (slab + 1) * nodes_x
    tail = r - (slab + 1) * nodes_x
    node_a = jnp.where(inner, r % nodes_x, nodes_x)
    node_b = jnp.where(inner, r // nodes_x, per_block * (tail % 8) + tail // 8)
    raw, total = node_weights(e1[...], o1[...], node_a + gx * nodes_x)
    wide = rows * depth
    pick = (
        iota((raw.shape[1], wide), 0) == gx * rows + iota((raw.shape[1], wide), 1) // depth
    ).astype(bf16)
    weight_x = expand(raw / total, pick)
    raw, total = node_weights(e3[...], o3[...], node_b + gz * slab)
    pick = (
        iota((raw.shape[1], wide), 0) == gz * depth + iota((raw.shape[1], wide), 1) % depth
    ).astype(bf16)
    weight_z = expand(raw / total, pick)
    k_high, k_low = split(weight_x * weight_z)
    k_both = jnp.concatenate([k_high, k_low], axis=0)

    lanes = 2 * per_block * nodes_y
    n = iota((lanes, 1), 0)
    mine = pl.ds(pl.multiple_of(gy * cols, cols), cols)
    spread = []
    for ghost in range(2):
        node = gy * nodes_y + (nodes_y if ghost else n % nodes_y)
        node = node + jnp.zeros_like(n)
        total = node_weights(e2[...], o2[...], node)[1]
        weight = node_weights(e2[:, mine], o2[:, mine], node)[0] / total
        if ghost:
            weight = jnp.where(n % nodes_y == 0, weight, 0.0)
        spread.append(
            jnp.concatenate(
                [
                    jnp.where(n // nodes_y == f * per_block + b, weight, 0.0)
                    for b in range(per_block)
                    for f in range(2)
                ],
                axis=1,
            )
        )
    y_high, y_low = split(jnp.concatenate(spread, axis=0))

    def to_message(values):
        high, low = split(values)
        dims = (((1,), (1,)), ((), ()))
        dot = functools.partial(
            lax.dot_general, dimension_numbers=dims, preferred_element_type=f32
        )
        return dot(high, y_high) + dot(low, y_high) + dot(high, y_low)

    def part(c):
        first = c * chunk * nodes_x
        last = (c + 1) * chunk * nodes_x + (nodes_x if c == CHUNKS - 1 else 0)
        return pl.ds(first, last - first)

    def main_copy(q, c):
        return pltpu.make_async_remote_copy(
            src_ref=main.at[q, part(c)],
            dst_ref=got_main.at[gy, part(c)],
            send_sem=send_main.at[q, c],
            recv_sem=recv_main.at[gy, c],
            device_id=(gx, gz, q),
            device_id_type=MESH,
        )

    def third_part(c):
        step = chunk // per_block * nodes_x
        return pl.ds(c * step, step + (nodes_x if c == CHUNKS - 1 else 0))

    def third_copy(c):
        return pltpu.make_async_remote_copy(
            src_ref=third.at[third_part(c)],
            dst_ref=got_third.at[gy, third_part(c)],
            send_sem=send_main.at[blocks, c],
            recv_sem=recv_third.at[gy, c],
            device_id=(gx, gz + 1, 0),
            device_id_type=MESH,
        )

    def first_copy(q):
        return pltpu.make_async_remote_copy(
            src_ref=edge.at[q],
            dst_ref=got_first.at[gy],
            send_sem=send_edge.at[q],
            recv_sem=recv_first.at[gy],
            device_id=(gx + 1, gz, q),
            device_id_type=MESH,
        )

    def corner_copy():
        return pltpu.make_async_remote_copy(
            src_ref=edge.at[blocks],
            dst_ref=got_corner.at[gy],
            send_sem=send_edge.at[blocks],
            recv_sem=recv_corner.at[gy],
            device_id=(gx + 1, gz + 1, 0),
            device_id_type=MESH,
        )

    third_here = jnp.logical_and(gz == 0, gy == 1)
    third_away = jnp.logical_and(has_next_z, jnp.logical_not(third_here))

    def each_main(c, do):
        for q in range(blocks):

            @pl.when(jnp.logical_not(jnp.logical_and(own, gz == q)))
            def _(q=q):
                do(main_copy(q, c))

        @pl.when(third_away)
        def _():
            do(third_copy(c))

    def each_edge(do):
        @pl.when(has_next_x)
        def _():
            for q in range(blocks):
                do(first_copy(q))

        @pl.when(jnp.logical_and(has_next_x, has_next_z))
        def _():
            do(corner_copy())

    packed = pair = None
    tile = nodes_x
    for c in range(CHUNKS):
        gathered = []
        for t in range(c * chunk, (c + 1) * chunk):
            for copy in load(t):
                copy.wait()
            field = jnp.concatenate(
                [xc[t].reshape(wide, cols), xa[t].reshape(wide, cols)], axis=1
            )
            high, low = split(field)
            both = jnp.dot(k_both, high, preferred_element_type=f32)
            node = (
                both[:row_count]
                + both[row_count:]
                + jnp.dot(k_high, low, preferred_element_type=f32)
            )
            sides = []
            for k in range(per_block):
                pieces = []
                for q in range(blocks + 1):
                    b = q * per_block + k
                    if b <= slab:
                        pieces.append(node[b * tile : (b + 1) * tile])
                    else:
                        pieces.append(jnp.zeros((tile, 2 * cols), f32))
                base = (slab + 1) * tile + 8 * k
                pieces.append(node[base : base + 8])
                sides.append(jnp.concatenate(pieces, axis=0))
            gathered.append(jnp.concatenate(sides, axis=1))
        result = to_message(jnp.concatenate(gathered, axis=0))
        per = (blocks + 1) * tile + 8
        for k, t in enumerate(range(c * chunk, (c + 1) * chunk)):
            values = result[k * per : (k + 1) * per]
            for q in range(blocks):
                main[q, t * tile : (t + 1) * tile] = values[q * tile : (q + 1) * tile, :lanes]
            for q in range(blocks + 1):
                row = (blocks + 1) * tile + q
                edge[q, t : t + 1] = values[row : row + 1, :lanes]
            above = values[blocks * tile : (blocks + 1) * tile, :lanes]
            place = t % per_block
            pair = pltpu.roll(above, place * nodes_y, 1) + pair if place else above
            if place == per_block - 1:
                at = t // per_block * tile
                third[at : at + tile] = pair
            ghost = values[:, lanes:]
            if t:
                ghost = pltpu.roll(ghost, t, 1)
            packed = ghost if packed is None else packed + ghost
        if c == CHUNKS - 1:
            for q in range(blocks):
                main[q, subs * tile : (subs + 1) * tile] = packed[q * tile : (q + 1) * tile]
            at = subs // per_block * tile
            third[at : at + tile] = packed[blocks * tile : (blocks + 1) * tile]
            for q in range(blocks + 1):
                row = (blocks + 1) * tile + q
                edge[q, subs : subs + 1] = packed[row : row + 1]
        if c == 0:
            count = blocks + has_next_z.astype(jnp.int32)
            count = count * jnp.where(has_next_x, 2, 1)
            count = count - jnp.logical_or(own, third_here).astype(jnp.int32)
            pl.semaphore_wait(barrier, count)
        each_main(c, lambda copy: copy.start())
    each_edge(lambda copy: copy.start())

    @pl.when(own)
    def _():
        got_main[gy] = main[gz]

    @pl.when(third_here)
    def _():
        got_third[gy] = third[...]

    for s in range(ny):

        @pl.when(jnp.logical_not(jnp.logical_and(own, gy == s)))
        def _(s=s):
            for c in range(CHUNKS):
                pltpu.make_async_remote_copy(
                    src_ref=main.at[0, part(c)],
                    dst_ref=got_main.at[s, part(c)],
                    send_sem=send_main.at[0, c],
                    recv_sem=recv_main.at[s, c],
                    device_id=(gx, gy, gz),
                    device_id_type=MESH,
                ).wait_recv()

    @pl.when(from_third)
    def _():
        for s in range(ny):

            @pl.when(jnp.logical_not(jnp.logical_and(gy == 1, jnp.logical_and(gz == 0, s == gy)) & (gz == gy - 1)))
            def _(s=s):
                for c in range(CHUNKS):
                    pltpu.make_async_remote_copy(
                        src_ref=third.at[third_part(c)],
                        dst_ref=got_third.at[s, third_part(c)],
                        send_sem=send_main.at[0, c],
                        recv_sem=recv_third.at[s, c],
                        device_id=(gx, gy, gz),
                        device_id_type=MESH,
                    ).wait_recv()

            first_block = iota((tile, lanes), 1) // nodes_y % per_block == 0
            for t in range(subs):
                at = t // per_block * tile
                moved = got_third[s, at : at + tile]
                place = t % per_block
                if place:
                    moved = pltpu.roll(moved, lanes - place * nodes_y, 1)
                rows_t = pl.ds(t * tile, tile)
                got_main[s, rows_t] = got_main[s, rows_t] + jnp.where(first_block, moved, 0.0)
            at = subs // per_block * tile
            rows_t = pl.ds(subs * tile, tile)
            got_main[s, rows_t] = got_main[s, rows_t] + got_third[s, at : at + tile]

    def add_edge(source, sem, s):
        pltpu.make_async_remote_copy(
            src_ref=edge.at[0],
            dst_ref=source.at[s],
            send_sem=send_edge.at[0],
            recv_sem=sem.at[s],
            device_id=(gx, gy, gz),
            device_id_type=MESH,
        ).wait_recv()
        for t in range(subs + 1):
            at = pl.ds(t * tile, 1)
            got_main[s, at] = got_main[s, at] + source[s, t : t + 1]

    @pl.when(from_first)
    def _():
        for s in range(ny):
            add_edge(got_first, recv_first, s)

    @pl.when(from_corner)
    def _():
        for s in range(ny):
            add_edge(got_corner, recv_corner, s)

    for copy in fetches[6:]:
        copy.wait()
    lane = iota((tile, lanes), 1)
    lane_y = iota((tile, all_y), 1)
    ghosts = [got_main[s, subs * tile : (subs + 1) * tile] for s in range(ny - 1)]
    bound = [troponin[:, k, :] for k in range(per_block)]
    active = [tension[:, k, :] for k in range(per_block)]
    unbind_rate = [unbind[:, k, :] for k in range(per_block)]
    relax_rate = [relax[:, k, :] for k in range(per_block)]
    for t in range(subs):
        pieces = []
        for s in range(ny):
            value = got_main[s, t * tile : (t + 1) * tile]
            if s:
                moved = pltpu.roll(ghosts[s - 1], lanes - t, 1) if t else ghosts[s - 1]
                value = value + jnp.where(lane % nodes_y == 0, moved, 0.0)
            pieces.append(value)

        def drive(f, k):
            at = (f * per_block + k) * nodes_y
            total = None
            for s in range(ny):
                shift = (s * nodes_y - at) % lanes
                moved = pltpu.roll(pieces[s], shift, 1) if shift else pieces[s]
                total = moved if total is None else jnp.where(lane_y // nodes_y == s, moved, total)
            return total

        for k in range(per_block):
            squared = drive(0, k)
            squared = squared * squared
            binding = squared / (squared + half_square)
            bound[k] = bound[k] + step_size * (
                bind_rate * binding * (1.0 - bound[k]) - unbind_rate[k] * bound[k]
            )
            active[k] = active[k] + step_size * relax_rate[k] * (
                peak_tension * drive(1, k) * bound[k] - active[k]
            )
    for k in range(per_block):
        out_bound[:, k, :] = bound[k]
        out_active[:, k, :] = active[k]

    for c in range(CHUNKS):
        each_main(c, lambda copy: copy.wait_send())
    each_edge(lambda copy: copy.wait_send())


def store_results(bound, active, out_bound, out_active, sem):
    copies = (
        pltpu.make_async_copy(bound, out_bound, sem.at[0]),
        pltpu.make_async_copy(active, out_active, sem.at[1]),
    )
    for copy in copies:
        copy.start()
    for copy in copies:
        copy.wait()


def per_device(calcium, activation, e1, o1, e2, o2, e3, o3, troponin, tension, unbind, relax, *, sizes):
    nx, ny, nz = sizes
    subs, rows, depth, cols = calcium.shape
    nodes_x, per_block, all_y = troponin.shape
    lanes = 2 * per_block * (all_y // ny)
    blocks = nz
    long = (subs + 1) * nodes_x
    short = (subs // per_block + 1) * nodes_x
    vmem = pl.BlockSpec(memory_space=pltpu.VMEM)
    hbm = pl.BlockSpec(memory_space=pltpu.MemorySpace.HBM)
    dma = pltpu.SemaphoreType.DMA
    flat = [x.reshape(1, -1) for x in (e1, o1, e2, o2, e3, o3)]
    shape = jax.ShapeDtypeStruct(troponin.shape, f32)
    operands = [
        pltpu.with_memory_space_constraint(x, pltpu.MemorySpace.HBM)
        for x in (calcium, activation, *flat, troponin, tension, unbind, relax)
    ]
    results = pl.pallas_call(
        functools.partial(kernel, sizes=sizes),
        out_shape=(shape, shape),
        in_specs=[hbm] * 12,
        out_specs=(vmem, vmem),
        scratch_shapes=[
            pltpu.VMEM(calcium.shape, f32),
            pltpu.VMEM(calcium.shape, f32),
            *[pltpu.VMEM(x.shape, x.dtype) for x in (*flat, troponin, tension, unbind, relax)],
            pltpu.VMEM((blocks, long, lanes), f32),
            pltpu.VMEM((short, lanes), f32),
            pltpu.VMEM((blocks + 1, subs + 1, lanes), f32),
            pltpu.VMEM((ny, long, lanes), f32),
            pltpu.VMEM((ny, short, lanes), f32),
            pltpu.VMEM((ny, subs + 1, lanes), f32),
            pltpu.VMEM((ny, subs + 1, lanes), f32),
            dma((2, subs)),
            dma((10,)),
            dma((blocks + 1, CHUNKS)),
            dma((blocks + 1,)),
            dma((ny, CHUNKS)),
            dma((ny, CHUNKS)),
            dma((ny,)),
            dma((ny,)),
        ],
        compiler_params=pltpu.CompilerParams(
            collective_id=0, has_side_effects=True, vmem_limit_bytes=32 * 1024 * 1024
        ),
        name="restrict_steps",
    )(*operands)
    results = [pltpu.with_memory_space_constraint(x, pltpu.MemorySpace.VMEM) for x in results]
    return pl.pallas_call(
        store_results,
        out_shape=(shape, shape),
        in_specs=[vmem] * 2,
        out_specs=(hbm, hbm),
        scratch_shapes=[dma((2,))],
        name="store_results",
    )(*results)


def solution(mesh):
    sizes = tuple(mesh.shape[name] for name in ("gx", "gy", "gz"))
    field = P(None, "gx", "gz", "gy")
    nodes = P("gx", ("gy", "gz"), None)
    return jax.shard_map(
        functools.partial(per_device, sizes=sizes),
        mesh=mesh,
        in_specs=(field, field, P(), P(), P(), P(), P(), P(), nodes, nodes, nodes, nodes),
        out_specs=(nodes, nodes),
        check_vma=False,
    )
```

profile of v0, /device:TPU:7, one launch (start us, length us, event | category | flops | bytes accessed | tf_op | source)
XLA Modules:
  0.0 18.0 jit_solution(6821359434113020723)
XLA Ops:
  0.6 16.8 %restrict_steps.1 = (f32[8,2,128]{2,1,0:T(2,128)S(1)}, f32[8,2,128]{2,1,0:T(2,128)S(1)}) custom-call(f32[8,32,32,128]{3,2,1,0:T(8,128)} %calcium.1, f32[8,32,32,128]{3,2,1,0:T(8,128)} %activation.1, s32[1,64]{1,0:T(1,128)} %bitcast.8, f32[1,64]{1,0:T(1,128)} %bitcast.9, s32[1,512]{1,0:T(1,128)} %bitcast.6, f32[1,512]{1,0:T(1,128)} %bitcast.7, ...), custom_call_target="tpu_custom_call" | custom-call | tf_op jit(solution)/shard_map/restrict_steps/pallas_call | solution.py:465
  17.4 0.6 %store_results.1 = (f32[8,2,128]{2,1,0:T(2,128)}, f32[8,2,128]{2,1,0:T(2,128)}) custom-call(f32[8,2,128]{2,1,0:T(2,128)S(1)} %get-tuple-element.4.bound, f32[8,2,128]{2,1,0:T(2,128)S(1)} %get-tuple-element.5.active), custom_call_target="tpu_custom_call" | custom-call | tf_op jit(solution)/shard_map/store_results/pallas_call | solution.py:496
where the time goes:
time: 18.2 us; the launch traced here: 18 us
  Pallas kernels  17.4 us (96%)
  between operations  0.64 us (4%)
    pallas_call x1, Pallas kernels, per_device(): pl.pallas_call(functools.partial(kernel, sizes=sizes), out_shape=(shape,...  16.8 us
    pallas_call x1, Pallas kernels, per_device(): pl.pallas_call(store_results, out_shape=(shape, shape), in_specs=[vmem] *...  0.62 us

commit v1 on v0

--- a/solution.py
+++ b/solution.py
@@ -91,7 +91,7 @@
         copy.start()
     for t in range(subs):
         for copy in load(t):
-            copy.start()
+            copy.start(priority=1)
 
     barrier = pltpu.get_barrier_semaphore()
     has_next_x = gx + 1 < nx

time: 18.2 us -> 16.7 us (0.918)
  Pallas kernels: 17.4 us -> 15.9 us
    pallas_call x1, Pallas kernels: 16.8 us -> 15.2 us  [per_device(): pl.pallas_call(functools.partial(kernel, sizes=sizes), out_shape=(shape,...]
where the time goes in v1:
time: 16.7 us; the launch traced here: 16.5 us
  Pallas kernels  15.9 us (95%)
  between operations  0.64 us (4%)
    pallas_call x1, Pallas kernels, per_device(): pl.pallas_call(functools.partial(kernel, sizes=sizes), out_shape=(shape,...  15.2 us
    pallas_call x1, Pallas kernels, per_device(): pl.pallas_call(store_results, out_shape=(shape, shape), in_specs=[vmem] *...  0.62 us

profile of v1, /device:TPU:7, one launch (start us, length us, event | category | flops | bytes accessed | tf_op | source)
XLA Modules:
  0.0 16.5 jit_solution(10639454404467506716)
XLA Ops:
  0.6 15.2 %restrict_steps.1 = (f32[8,2,128]{2,1,0:T(2,128)S(1)}, f32[8,2,128]{2,1,0:T(2,128)S(1)}) custom-call(f32[8,32,32,128]{3,2,1,0:T(8,128)} %calcium.1, f32[8,32,32,128]{3,2,1,0:T(8,128)} %activation.1, s32[1,64]{1,0:T(1,128)} %bitcast.8, f32[1,64]{1,0:T(1,128)} %bitcast.9, s32[1,512]{1,0:T(1,128)} %bitcast.6, f32[1,512]{1,0:T(1,128)} %bitcast.7, ...), custom_call_target="tpu_custom_call" | custom-call | tf_op jit(solution)/shard_map/restrict_steps/pallas_call | solution.py:465
  15.9 0.6 %store_results.1 = (f32[8,2,128]{2,1,0:T(2,128)}, f32[8,2,128]{2,1,0:T(2,128)}) custom-call(f32[8,2,128]{2,1,0:T(2,128)S(1)} %get-tuple-element.4.bound, f32[8,2,128]{2,1,0:T(2,128)S(1)} %get-tuple-element.5.active), custom_call_target="tpu_custom_call" | custom-call | tf_op jit(solution)/shard_map/store_results/pallas_call | solution.py:496

commit v2 on v1

--- a/solution.py
+++ b/solution.py
@@ -58,6 +58,7 @@
         got_third,
         got_first,
         got_corner,
+        relay,
         load_sem,
         small_sem,
         send_main,
@@ -66,6 +67,8 @@
         recv_third,
         recv_first,
         recv_corner,
+        send_relay,
+        recv_relay,
     ) = refs[24:]
     e1, o1, e2, o2, e3, o3, troponin, tension, unbind, relax = local
     nx, ny, nz = sizes
@@ -100,6 +103,24 @@
     from_third = jnp.logical_and(gz == 0, gy > 0)
     from_first = gx > 0
     from_corner = jnp.logical_and(from_third, from_first)
+    half = blocks // 2
+    column = gz // half
+    home = gy // half
+    last = gz % half == half - 1
+    crossing = column != home
+
+    def hello(*device):
+        pl.semaphore_signal(barrier, inc=1, device_id=device, device_id_type=MESH)
+
+    def far_slabs(do):
+        for i in range(half):
+            slab_i = (1 - column) * half + i
+
+            @pl.when(jnp.logical_and(last, slab_i != gy))
+            def _(i=i, slab_i=slab_i):
+                do(i, slab_i)
+
+    far_slabs(lambda i, slab_i: hello(gx, gy, slab_i))
     for s in range(ny):
 
         def greet(dx, dz, s=s):
@@ -107,9 +128,17 @@
                 barrier, inc=1, device_id=(gx - dx, s, gy - dz), device_id_type=MESH
             )
 
-        @pl.when(jnp.logical_not(jnp.logical_and(s == gy, own)))
+        @pl.when(jnp.logical_and(jnp.logical_not(crossing), jnp.logical_not(jnp.logical_and(s == gy, own))))
         def _():
             greet(0, 0)
+
+        @pl.when(jnp.logical_and(crossing, s == gy))
+        def _():
+            greet(0, 0)
+
+        @pl.when(jnp.logical_and(crossing, s != gy))
+        def _(s=s):
+            hello(gx, s, column * half + half - 1)
 
         @pl.when(jnp.logical_and(from_third, jnp.logical_not(jnp.logical_and(s == gy, gy - 1 == gz))))
         def _():
@@ -191,6 +220,26 @@
             device_id_type=MESH,
         )
 
+    def hand_over(q, c):
+        return pltpu.make_async_remote_copy(
+            src_ref=main.at[q, part(c)],
+            dst_ref=relay.at[gz % half, q % half, part(c)],
+            send_sem=send_main.at[q, c],
+            recv_sem=recv_relay.at[gz % half, q % half, c],
+            device_id=(gx, gy, q // half * half + half - 1),
+            device_id_type=MESH,
+        )
+
+    def forward(i, slab_i, j, c):
+        return pltpu.make_async_remote_copy(
+            src_ref=relay.at[i, j, part(c)],
+            dst_ref=got_main.at[gy, part(c)],
+            send_sem=send_relay.at[i, j, c],
+            recv_sem=recv_main.at[gy, c],
+            device_id=(gx, slab_i, column * half + j),
+            device_id_type=MESH,
+        )
+
     def third_part(c):
         step = chunk // per_block * nodes_x
         return pl.ds(c * step, step + (nodes_x if c == CHUNKS - 1 else 0))
@@ -231,9 +280,13 @@
     def each_main(c, do):
         for q in range(blocks):
 
-            @pl.when(jnp.logical_not(jnp.logical_and(own, gz == q)))
+            @pl.when(jnp.where(own, gz != q, column == q // half))
             def _(q=q):
                 do(main_copy(q, c))
+
+            @pl.when(jnp.logical_and(jnp.logical_not(own), column != q // half))
+            def _(q=q):
+                do(hand_over(q, c))
 
         @pl.when(third_away)
         def _():
@@ -307,12 +360,33 @@
                 row = (blocks + 1) * tile + q
                 edge[q, subs : subs + 1] = packed[row : row + 1]
         if c == 0:
-            count = blocks + has_next_z.astype(jnp.int32)
-            count = count * jnp.where(has_next_x, 2, 1)
-            count = count - jnp.logical_or(own, third_here).astype(jnp.int32)
+            extra = blocks + has_next_z.astype(jnp.int32)
+            count = jnp.where(has_next_x, extra, 0)
+            count = count + jnp.where(own, blocks - 1, half + 1)
+            count = count + third_away.astype(jnp.int32)
+            served = half - crossing.astype(jnp.int32)
+            count = count + jnp.where(last, served * half, 0)
             pl.semaphore_wait(barrier, count)
         each_main(c, lambda copy: copy.start())
     each_edge(lambda copy: copy.start())
+
+    def pass_on(c):
+        def one(i, slab_i):
+            for j in range(half):
+                pltpu.make_async_remote_copy(
+                    src_ref=main.at[0, part(c)],
+                    dst_ref=relay.at[i, j, part(c)],
+                    send_sem=send_main.at[0, c],
+                    recv_sem=recv_relay.at[i, j, c],
+                    device_id=(gx, gy, gz),
+                    device_id_type=MESH,
+                ).wait_recv()
+                forward(i, slab_i, j, c).start()
+
+        far_slabs(one)
+
+    for c in range(CHUNKS):
+        pass_on(c)
 
     @pl.when(own)
     def _():
@@ -431,6 +505,11 @@
 
     for c in range(CHUNKS):
         each_main(c, lambda copy: copy.wait_send())
+        def sent(i, slab_i, c=c):
+            for j in range(half):
+                forward(i, slab_i, j, c).wait_send()
+
+        far_slabs(sent)
     each_edge(lambda copy: copy.wait_send())
 
 
@@ -478,6 +557,7 @@
             pltpu.VMEM((ny, short, lanes), f32),
             pltpu.VMEM((ny, subs + 1, lanes), f32),
             pltpu.VMEM((ny, subs + 1, lanes), f32),
+            pltpu.VMEM((blocks // 2, blocks // 2, long, lanes), f32),
             dma((2, subs)),
             dma((10,)),
             dma((blocks + 1, CHUNKS)),
@@ -486,6 +566,8 @@
             dma((ny, CHUNKS)),
             dma((ny,)),
             dma((ny,)),
+            dma((blocks // 2, blocks // 2, CHUNKS)),
+            dma((blocks // 2, blocks // 2, CHUNKS)),
         ],
         compiler_params=pltpu.CompilerParams(
             collective_id=0, has_side_effects=True, vmem_limit_bytes=32 * 1024 * 1024

time: 16.7 us -> 15.1 us (0.904)
  Pallas kernels: 15.9 us -> 14.4 us
    pallas_call x1, Pallas kernels: 15.2 us -> 13.7 us  [per_device(): pl.pallas_call(functools.partial(kernel, sizes=sizes), out_shape=(shape,...]
where the time goes in v2:
time: 15.1 us; the launch traced here: 15 us
  Pallas kernels  14.4 us (95%)
  between operations  0.64 us (4%)
    pallas_call x1, Pallas kernels, per_device(): pl.pallas_call(functools.partial(kernel, sizes=sizes), out_shape=(shape,...  13.7 us
    pallas_call x1, Pallas kernels, per_device(): pl.pallas_call(store_results, out_shape=(shape, shape), in_specs=[vmem] *...  0.62 us

profile of v2, /device:TPU:7, one launch (start us, length us, event | category | flops | bytes accessed | tf_op | source)
XLA Modules:
  0.0 15.0 jit_solution(2393771599677132764)
XLA Ops:
  0.6 13.7 %restrict_steps.1 = (f32[8,2,128]{2,1,0:T(2,128)S(1)}, f32[8,2,128]{2,1,0:T(2,128)S(1)}) custom-call(f32[8,32,32,128]{3,2,1,0:T(8,128)} %calcium.1, f32[8,32,32,128]{3,2,1,0:T(8,128)} %activation.1, s32[1,64]{1,0:T(1,128)} %bitcast.8, f32[1,64]{1,0:T(1,128)} %bitcast.9, s32[1,512]{1,0:T(1,128)} %bitcast.6, f32[1,512]{1,0:T(1,128)} %bitcast.7, ...), custom_call_target="tpu_custom_call" | custom-call | tf_op jit(solution)/shard_map/restrict_steps/pallas_call | solution.py:544
  14.4 0.6 %store_results.1 = (f32[8,2,128]{2,1,0:T(2,128)}, f32[8,2,128]{2,1,0:T(2,128)}) custom-call(f32[8,2,128]{2,1,0:T(2,128)S(1)} %get-tuple-element.4.bound, f32[8,2,128]{2,1,0:T(2,128)S(1)} %get-tuple-element.5.active), custom_call_target="tpu_custom_call" | custom-call | tf_op jit(solution)/shard_map/store_results/pallas_call | solution.py:578

commit v3 on v2

v3 whole, which is shorter than its diff:
```python
import functools

import jax
import jax.numpy as jnp
from jax import lax
from jax.experimental import pallas as pl
from jax.experimental.pallas import tpu as pltpu
from jax.sharding import PartitionSpec as P

step_size = 0.2
bind_rate = 2.0
peak_tension = 2.0
half_square = 0.25
f32 = jnp.float32
bf16 = jnp.bfloat16
MESH = pl.DeviceIdType.MESH


def split(x):
    high = x.astype(bf16)
    return high, (x - high.astype(f32)).astype(bf16)


def node_weights(element, offset, node):
    raw = jnp.where(element == node, 1.0 - offset, 0.0) + jnp.where(
        element + 1 == node, offset, 0.0
    )
    total = jnp.sum(raw, axis=1, keepdims=True)
    return raw, jnp.where(total > 0.0, total, 1.0)


def expand(weight, pick):
    high, low = split(weight)
    return jnp.dot(high, pick, preferred_element_type=f32) + jnp.dot(
        low, pick, preferred_element_type=f32
    )


def iota(shape, dim):
    return lax.broadcasted_iota(jnp.int32, shape, dim)


def kernel(
    calcium,
    activation,
    *refs,
    sizes,
):
    small = refs[:10]
    out_bound, out_active, x = refs[10:13]
    local = refs[13:23]
    (
        main,
        third,
        edge,
        got_main,
        got_third,
        got_edge,
        pool,
        send_relay,
        recv_main,
        recv_third,
        recv_edge,
    ) = refs[23:]
    e1, o1, e2, o2, e3, o3, troponin, tension, unbind, relax = local
    nx, ny, nz = sizes
    _, subs, rows, depth, cols = x.shape
    nodes_x, per_block, all_y = troponin.shape
    nodes_y = all_y // ny
    blocks = nz
    slab = per_block * blocks
    gx, gy, gz = lax.axis_index("gx"), lax.axis_index("gy"), lax.axis_index("gz")
    groups = [[t, t + 1] for t in range(0, subs, 2)]
    cuts = [group[-1] + 1 for group in groups]
    chunks = len(cuts)

    def load(t):
        at = len(small) + t
        return [
            pltpu.make_async_copy(field.at[t], x.at[f, t], pool.at[at])
            for f, field in enumerate((calcium, activation))
        ]

    def loaded(t):
        at = len(small) + t
        pltpu.make_async_copy(calcium.at[pl.ds(0, 2)], x.at[:, t], pool.at[at]).wait()

    fetches = [
        pltpu.make_async_copy(source, target, pool.at[i])
        for i, (source, target) in enumerate(zip(small, local))
    ]
    for copy in fetches:
        copy.start()
    for t in range(subs):
        for copy in load(t):
            copy.start(priority=1)

    barrier = pltpu.get_barrier_semaphore()
    has_next_x = gx + 1 < nx
    has_next_z = gz + 1 < nz
    own = gy == gz
    from_third = jnp.logical_and(gz == 0, gy > 0)
    from_first = gx > 0
    from_corner = jnp.logical_and(from_third, from_first)
    half = blocks // 2
    column = gz // half
    home = gy // half
    last = gz % half == half - 1
    crossing = column != home

    def hello(*device):
        pl.semaphore_signal(barrier, inc=1, device_id=device, device_id_type=MESH)

    def far_slabs(do):
        for i in range(half):
            slab_i = (1 - column) * half + i

            @pl.when(jnp.logical_and(last, slab_i != gy))
            def _(i=i, slab_i=slab_i):
                do(i, slab_i)

    far_slabs(lambda i, slab_i: hello(gx, gy, slab_i))
    for s in range(ny):

        def greet(dx, dz, s=s):
            pl.semaphore_signal(
                barrier, inc=1, device_id=(gx - dx, s, gy - dz), device_id_type=MESH
            )

        @pl.when(jnp.logical_and(jnp.logical_not(crossing), jnp.logical_not(jnp.logical_and(s == gy, own))))
        def _():
            greet(0, 0)

        @pl.when(jnp.logical_and(crossing, s == gy))
        def _():
            greet(0, 0)

        @pl.when(jnp.logical_and(crossing, s != gy))
        def _(s=s):
            hello(gx, s, column * half + half - 1)

        @pl.when(jnp.logical_and(from_third, jnp.logical_not(jnp.logical_and(s == gy, gy - 1 == gz))))
        def _():
            greet(0, 1)

        @pl.when(from_first)
        def _():
            greet(1, 0)

        @pl.when(from_corner)
        def _():
            greet(1, 1)

    for copy in fetches[:6]:
        copy.wait()
    tile = nodes_x
    seg = per_block * nodes_y
    lanes = 2 * seg
    first_side = (blocks + 2) * tile
    other_side = (blocks + 1) * tile
    row_count = first_side + (per_block - 1) * other_side
    r = iota((row_count, 1), 0)
    side = jnp.where(r < first_side, 0, (r - first_side) // other_side + 1)
    place = jnp.where(r < first_side, r, (r - first_side) % other_side)
    inner = place < jnp.where(r < first_side, first_side, other_side) - tile
    node_a = jnp.where(inner, place % tile, nodes_x)
    node_b = per_block * jnp.where(inner, place // tile, place % tile) + side
    raw, total = node_weights(e1[...], o1[...], node_a + gx * nodes_x)
    wide = rows * depth
    pick = (
        iota((raw.shape[1], wide), 0) == gx * rows + iota((raw.shape[1], wide), 1) // depth
    ).astype(bf16)
    weight_x = expand(raw / total, pick)
    raw, total = node_weights(e3[...], o3[...], node_b + gz * slab)
    pick = (
        iota((raw.shape[1], wide), 0) == gz * depth + iota((raw.shape[1], wide), 1) % depth
    ).astype(bf16)
    weight_z = expand(raw / total, pick)
    k_high, k_low = split(weight_x * weight_z)
    k_both = jnp.concatenate([k_high, k_low], axis=0)

    def y_weights():
        n = iota((lanes, 1), 0)
        mine = pl.ds(pl.multiple_of(gy * cols, cols), cols)
        spot = n % seg
        beyond = jnp.logical_and(spot >= nodes_y, spot % subs == nodes_y % subs)
        beyond = jnp.logical_and(beyond, spot < nodes_y + per_block * subs)
        node = gy * nodes_y + jnp.where(spot < nodes_y, spot, nodes_y)
        total = node_weights(e2[...], o2[...], node)[1]
        weight = node_weights(e2[:, mine], o2[:, mine], node)[0] / total
        weight = jnp.where(jnp.logical_or(spot < nodes_y, beyond), weight, 0.0).T
        field = iota(weight.shape, 1) // seg
        weight = jnp.concatenate([jnp.where(field == f, weight, 0.0) for f in range(2)], axis=0)
        return jnp.concatenate(split(weight), axis=1)

    def to_message(node, y_both):
        count = node.shape[0]
        out = jnp.dot(
            jnp.concatenate(split(node), axis=0), y_both, preferred_element_type=f32
        )
        return out[:count, :lanes] + out[:count, lanes:] + out[count:, :lanes]

    def span(first, last):
        stop = last * tile + (tile if last == subs else 0)
        return pl.ds(first * tile, stop - first * tile)

    def part(c):
        return span(cuts[c - 1] if c else 0, cuts[c])

    def main_copy(q, c):
        where = part(c) if c < chunks else span(0, subs)
        direct = jnp.logical_or(own, column == q // half).astype(jnp.int32)
        over = 1 - direct
        slot = gz % half * half + q % half
        return pltpu.make_async_remote_copy(
            src_ref=main.at[q, where],
            dst_ref=got_main.at[direct * gy + over * (ny + slot), where],
            send_sem=pool.at[q],
            recv_sem=recv_main.at[direct * gy + over * (ny + slot * chunks + c % chunks)],
            device_id=(
                gx,
                direct * gz + over * gy,
                direct * q + over * (q // half * half + half - 1),
            ),
            device_id_type=MESH,
        )

    def forward(i, slab_i, j, c):
        where = part(c) if c < chunks else span(0, subs)
        return pltpu.make_async_remote_copy(
            src_ref=got_main.at[ny + i * half + j, where],
            dst_ref=got_main.at[gy, where],
            send_sem=send_relay.at[i, j],
            recv_sem=recv_main.at[gy],
            device_id=(gx, slab_i, column * half + j),
            device_id_type=MESH,
        )

    def third_copy(where):
        return pltpu.make_async_remote_copy(
            src_ref=third.at[where],
            dst_ref=got_third.at[gy, where],
            send_sem=pool.at[blocks],
            recv_sem=recv_third.at[gy],
            device_id=(gx, gz + 1, 0),
            device_id_type=MESH,
        )

    def edge_copy(q, corner):
        return pltpu.make_async_remote_copy(
            src_ref=edge.at[q],
            dst_ref=got_edge.at[gy, corner],
            send_sem=pool.at[len(small) + q],
            recv_sem=recv_edge.at[gy],
            device_id=(gx + 1, gz + corner, 0 if corner else q),
            device_id_type=MESH,
        )

    third_here = jnp.logical_and(gz == 0, gy == 1)
    third_away = jnp.logical_and(has_next_z, jnp.logical_not(third_here))

    def each_main(do, c, up):
        for q in range(blocks):

            @pl.when(jnp.logical_not(jnp.logical_and(own, gz == q)))
            def _(q=q):
                do(main_copy(q, c))

        if up.size:

            @pl.when(third_away)
            def _():
                do(third_copy(up))

    def send(c):
        pairs = [cut // per_block * tile for cut in (cuts[c - 1] if c else 0, cuts[c])]
        pairs[1] += tile if c == chunks - 1 else 0
        each_main(lambda copy: copy.start(), c, pl.ds(pairs[0], pairs[1] - pairs[0]))

    def each_edge(do):
        @pl.when(has_next_x)
        def _():
            for q in range(blocks):
                do(edge_copy(q, 0))

        @pl.when(jnp.logical_and(has_next_x, has_next_z))
        def _():
            do(edge_copy(blocks, 1))

    spot = iota((tile, lanes), 1) % seg
    pieces = blocks + 2
    state = {"packed": None, "pair": None}

    def nodes_of(group):
        fields = [x[f, t].reshape(wide, cols) for t in group for f in range(2)]
        high, low = split(jnp.concatenate(fields, axis=1))
        both = jnp.dot(k_both, high, preferred_element_type=f32)
        node = (
            both[:row_count]
            + both[row_count:]
            + jnp.dot(k_high, low, preferred_element_type=f32)
        )
        width = 2 * cols
        return jnp.concatenate(
            [node[:, i * width : (i + 1) * width] for i in range(len(group))], axis=0
        )

    def place_message(t, values):
        main_tiles, ghost_tiles = [], []
        for i in range(pieces):
            total, ghost = values[i * tile : (i + 1) * tile], 0.0
            here = total
            for k in range(per_block):
                if k and i == blocks:
                    here = None
                elif k:
                    at = first_side + (k - 1) * other_side + (i - (i > blocks)) * tile
                    here = values[at : at + tile]
                in_place = spot // nodes_y == k
                if k:
                    total = jnp.where(in_place, 0.0 if here is None else pltpu.roll(here, k * nodes_y, 1), total)
                if here is not None:
                    ghost = jnp.where(spot == nodes_y + k * subs, here, ghost)
            main_tiles.append(total)
            ghost_tiles.append(pltpu.roll(ghost, t, 1) if t else ghost)
        for q in range(blocks):
            main[q, t * tile : (t + 1) * tile] = main_tiles[q]
        for q in range(blocks + 1):
            edge[q, t : t + 1] = main_tiles[blocks + 1][q : q + 1]
        above = main_tiles[blocks]
        fold = t % per_block
        state["pair"] = pltpu.roll(above, fold * nodes_y, 1) + state["pair"] if fold else above
        if fold == per_block - 1:
            at = t // per_block * tile
            third[at : at + tile] = state["pair"]
        packed = state["packed"]
        packed = ghost_tiles if packed is None else [x + y for x, y in zip(packed, ghost_tiles)]
        state["packed"] = packed
        if t == subs - 1:
            for q in range(blocks):
                main[q, subs * tile : (subs + 1) * tile] = packed[q]
            at = subs // per_block * tile
            third[at : at + tile] = packed[blocks]
            for q in range(blocks + 1):
                edge[q, subs : subs + 1] = packed[blocks + 1][q : q + 1]

    y_both = node = None
    for g in range(len(groups) + 1):
        group = groups[g] if g < len(groups) else []
        for t in group:
            loaded(t)
        before, node = node, nodes_of(group) if group else None
        if g == 0:
            y_both = y_weights()
            continue
        values = to_message(before, y_both)
        for i, t in enumerate(groups[g - 1]):
            place_message(t, values[i * row_count : (i + 1) * row_count])
        c = g - 1
        if c == 0:
            extra = blocks + has_next_z.astype(jnp.int32)
            count = jnp.where(has_next_x, extra, 0)
            count = count + jnp.where(own, blocks - 1, half + 1)
            count = count + third_away.astype(jnp.int32)
            served = half - crossing.astype(jnp.int32)
            count = count + jnp.where(last, served * half, 0)
            pl.semaphore_wait(barrier, count)
        send(c)
    each_edge(lambda copy: copy.start())

    for copy in fetches[6:]:
        copy.wait()

    def pass_on(i, slab_i):
        for c in range(chunks):
            for j in range(half):
                slot = i * half + j
                pltpu.make_async_remote_copy(
                    src_ref=main.at[0, part(c)],
                    dst_ref=got_main.at[ny + slot, part(c)],
                    send_sem=pool.at[0],
                    recv_sem=recv_main.at[ny + slot * chunks + c],
                    device_id=(gx, gy, gz),
                    device_id_type=MESH,
                ).wait_recv()
                forward(i, slab_i, j, c).start()

    far_slabs(pass_on)

    @pl.when(own)
    def _():
        got_main[gy] = main[gz]

    @pl.when(third_here)
    def _():
        got_third[gy] = third[...]

    for s in range(ny):

        @pl.when(jnp.logical_not(jnp.logical_and(own, gy == s)))
        def _(s=s):
            pltpu.make_async_remote_copy(
                src_ref=main.at[0],
                dst_ref=got_main.at[s],
                send_sem=pool.at[0],
                recv_sem=recv_main.at[s],
                device_id=(gx, gy, gz),
                device_id_type=MESH,
            ).wait_recv()

    @pl.when(from_third)
    def _():
        for s in range(ny):

            @pl.when(jnp.logical_not(jnp.logical_and(gy == 1, jnp.logical_and(gz == 0, s == gy)) & (gz == gy - 1)))
            def _(s=s):
                pltpu.make_async_remote_copy(
                    src_ref=third,
                    dst_ref=got_third.at[s],
                    send_sem=pool.at[0],
                    recv_sem=recv_third.at[s],
                    device_id=(gx, gy, gz),
                    device_id_type=MESH,
                ).wait_recv()

            first_block = iota((tile, lanes), 1) // nodes_y % per_block == 0
            for t in range(subs):
                at = t // per_block * tile
                moved = got_third[s, at : at + tile]
                place = t % per_block
                if place:
                    moved = pltpu.roll(moved, lanes - place * nodes_y, 1)
                rows_t = pl.ds(t * tile, tile)
                got_main[s, rows_t] = got_main[s, rows_t] + jnp.where(first_block, moved, 0.0)
            at = subs // per_block * tile
            rows_t = pl.ds(subs * tile, tile)
            got_main[s, rows_t] = got_main[s, rows_t] + got_third[s, at : at + tile]

    def add_edge(corners):
        for s in range(ny):
            pltpu.make_async_remote_copy(
                src_ref=edge.at[pl.ds(0, 1 + corners)],
                dst_ref=got_edge.at[s, pl.ds(0, 1 + corners)],
                send_sem=pool.at[0],
                recv_sem=recv_edge.at[s],
                device_id=(gx, gy, gz),
                device_id_type=MESH,
            ).wait_recv()
            for t in range(subs + 1):
                at = pl.ds(t * tile, 1)
                total = got_main[s, at]
                for corner in range(1 + corners):
                    total = total + got_edge[s, corner, t : t + 1]
                got_main[s, at] = total

    @pl.when(jnp.logical_and(from_first, jnp.logical_not(from_corner)))
    def _():
        add_edge(0)

    @pl.when(from_corner)
    def _():
        add_edge(1)

    lane = iota((tile, lanes), 1)
    lane_y = iota((tile, all_y), 1)
    ghosts = []
    for s in range(ny - 1):
        raw = got_main[s, subs * tile : (subs + 1) * tile]
        ghost = pltpu.roll(raw, lanes - nodes_y, 1)
        for k in range(1, per_block):
            moved = pltpu.roll(raw, (lanes + k * nodes_y - nodes_y - k * subs) % lanes, 1)
            ghost = jnp.where(spot // nodes_y == k, moved, ghost)
        ghosts.append(ghost)
    bound = [troponin[:, k, :] for k in range(per_block)]
    active = [tension[:, k, :] for k in range(per_block)]
    unbind_rate = [unbind[:, k, :] for k in range(per_block)]
    relax_rate = [relax[:, k, :] for k in range(per_block)]
    for t in range(subs):
        pieces = []
        for s in range(ny):
            value = got_main[s, t * tile : (t + 1) * tile]
            if s:
                moved = pltpu.roll(ghosts[s - 1], lanes - t, 1) if t else ghosts[s - 1]
                value = value + jnp.where(lane % nodes_y == 0, moved, 0.0)
            pieces.append(value)

        def drive(f, k):
            at = (f * per_block + k) * nodes_y
            total = None
            for s in range(ny):
                shift = (s * nodes_y - at) % lanes
                moved = pltpu.roll(pieces[s], shift, 1) if shift else pieces[s]
                total = moved if total is None else jnp.where(lane_y // nodes_y == s, moved, total)
            return total

        for k in range(per_block):
            squared = drive(0, k)
            squared = squared * squared
            binding = squared / (squared + half_square)
            bound[k] = bound[k] + step_size * (
                bind_rate * binding * (1.0 - bound[k]) - unbind_rate[k] * bound[k]
            )
            active[k] = active[k] + step_size * relax_rate[k] * (
                peak_tension * drive(1, k) * bound[k] - active[k]
            )
    for k in range(per_block):
        out_bound[:, k, :] = bound[k]
        out_active[:, k, :] = active[k]

    each_main(lambda copy: copy.wait_send(), chunks, pl.ds(0, third.shape[0]))
    each_edge(lambda copy: copy.wait_send())

    def sent(i, slab_i):
        for j in range(half):
            forward(i, slab_i, j, chunks).wait_send()

    far_slabs(sent)


def store_results(bound, active, out_bound, out_active, sem):
    copies = (
        pltpu.make_async_copy(bound, out_bound, sem.at[0]),
        pltpu.make_async_copy(active, out_active, sem.at[1]),
    )
    for copy in copies:
        copy.start()
    for copy in copies:
        copy.wait()


def per_device(calcium, activation, e1, o1, e2, o2, e3, o3, troponin, tension, unbind, relax, *, sizes):
    nx, ny, nz = sizes
    subs, rows, depth, cols = calcium.shape
    nodes_x, per_block, all_y = troponin.shape
    lanes = 2 * per_block * (all_y // ny)
    blocks = nz
    long = (subs + 1) * nodes_x
    short = (subs // per_block + 1) * nodes_x
    vmem = pl.BlockSpec(memory_space=pltpu.VMEM)
    hbm = pl.BlockSpec(memory_space=pltpu.MemorySpace.HBM)
    dma = pltpu.SemaphoreType.DMA
    flat = [x.reshape(1, -1) for x in (e1, o1, e2, o2, e3, o3)]
    shape = jax.ShapeDtypeStruct(troponin.shape, f32)
    operands = [
        pltpu.with_memory_space_constraint(x, pltpu.MemorySpace.HBM)
        for x in (calcium, activation, *flat, troponin, tension, unbind, relax)
    ]
    results = pl.pallas_call(
        functools.partial(kernel, sizes=sizes),
        out_shape=(shape, shape),
        in_specs=[hbm] * 12,
        out_specs=(vmem, vmem),
        scratch_shapes=[
            pltpu.VMEM((2, *calcium.shape), f32),
            *[pltpu.VMEM(x.shape, x.dtype) for x in (*flat, troponin, tension, unbind, relax)],
            pltpu.VMEM((blocks, long, lanes), f32),
            pltpu.VMEM((short, lanes), f32),
            pltpu.VMEM((blocks + 1, subs + 1, lanes), f32),
            pltpu.VMEM((ny + (blocks // 2) ** 2, long, lanes), f32),
            pltpu.VMEM((ny, short, lanes), f32),
            pltpu.VMEM((ny, 2, subs + 1, lanes), f32),
            dma((10 + subs,)),
            dma((blocks // 2, blocks // 2)),
            dma((ny + (blocks // 2) ** 2 * (subs // 2),)),
            dma((ny,)),
            dma((ny,)),
        ],
        compiler_params=pltpu.CompilerParams(
            collective_id=0, has_side_effects=True, vmem_limit_bytes=32 * 1024 * 1024
        ),
        name="restrict_steps",
    )(*operands)
    results = [pltpu.with_memory_space_constraint(x, pltpu.MemorySpace.VMEM) for x in results]
    return pl.pallas_call(
        store_results,
        out_shape=(shape, shape),
        in_specs=[vmem] * 2,
        out_specs=(hbm, hbm),
        scratch_shapes=[dma((2,))],
        name="store_results",
    )(*results)


def solution(mesh):
    sizes = tuple(mesh.shape[name] for name in ("gx", "gy", "gz"))
    field = P(None, "gx", "gz", "gy")
    nodes = P("gx", ("gy", "gz"), None)
    return jax.shard_map(
        functools.partial(per_device, sizes=sizes),
        mesh=mesh,
        in_specs=(field, field, P(), P(), P(), P(), P(), P(), nodes, nodes, nodes, nodes),
        out_specs=(nodes, nodes),
        check_vma=False,
    )
```

time: 15.1 us -> 14.8 us (0.980)
  the two profiles are of different devices: /device:TPU:7 before, /device:TPU:0 now
where the time goes in v3:
time: 14.8 us; the launch traced here: 14.6 us
  Pallas kernels  14 us (95%)
  between operations  0.64 us (4%)
    pallas_call x1, Pallas kernels, per_device(): pl.pallas_call(functools.partial(kernel, sizes=sizes), out_shape=(shape,...  13.4 us
    pallas_call x1, Pallas kernels, per_device(): pl.pallas_call(store_results, out_shape=(shape, shape), in_specs=[vmem] *...  0.62 us

profile of v3, /device:TPU:0, one launch (start us, length us, event | category | flops | bytes accessed | tf_op | source)
XLA Modules:
  0.0 14.6 jit_solution(9230497418008702274)
XLA Ops:
  0.6 13.4 %restrict_steps.1 = (f32[8,2,128]{2,1,0:T(2,128)S(1)}, f32[8,2,128]{2,1,0:T(2,128)S(1)}) custom-call(f32[8,32,32,128]{3,2,1,0:T(8,128)} %calcium.1, f32[8,32,32,128]{3,2,1,0:T(8,128)} %activation.1, s32[1,64]{1,0:T(1,128)} %bitcast.8, f32[1,64]{1,0:T(1,128)} %bitcast.9, s32[1,512]{1,0:T(1,128)} %bitcast.6, f32[1,512]{1,0:T(1,128)} %bitcast.7, ...), custom_call_target="tpu_custom_call" | custom-call | tf_op jit(solution)/shard_map/restrict_steps/pallas_call | solution.py:548
  14.0 0.6 %store_results.1 = (f32[8,2,128]{2,1,0:T(2,128)}, f32[8,2,128]{2,1,0:T(2,128)}) custom-call(f32[8,2,128]{2,1,0:T(2,128)S(1)} %get-tuple-element.4.bound, f32[8,2,128]{2,1,0:T(2,128)S(1)} %get-tuple-element.5.active), custom_call_target="tpu_custom_call" | custom-call | tf_op jit(solution)/shard_map/store_results/pallas_call | solution.py:574
